TPU v7x, 32 devices: a whole 2x2x4 slice. The times are simulated.
32 devices in a mesh: gx: 8 (over y, x, core), gy: 4 (over z).
Axes of the slice: x: 2, y: 2, z: 4, core: 2. Of those that a mesh axis runs over, the one named last changes fastest.
Arguments:
- estimate: float32 [128, 64, 128], P('gx', 'gy'), may hold values from 0.5 to 12
- recorded: float32 [2, 128, 64, 128], P(None, 'gx', 'gy'), may hold values from 0.1 to 3
- spread: float32 [2, 35937], replicated, may hold values from 2.7826474e-06 to 2.4
- background: float32 [2], replicated, may hold values from 0.2 to 1
Outputs:
- restored: float32 [128, 64, 128], P('gx', 'gy')
All inputs are finite; a program needn't handle non-finite values.
Results may differ from a plain program's by a relative error of at most 0.0001.
Values sent between devices are 32-bit elements; how exact they have to be, the bound alone decides.
A program may use at most 64 MiB of HBM per device.

v0:
```python
import functools
import math

import jax
import jax.numpy as jnp
import numpy as np
from jax import lax
from jax.experimental import pallas as pl
from jax.experimental.pallas import tpu as pltpu
from jax.sharding import PartitionSpec as P

clip_fraction = 0.6
F32 = jnp.float32
BF16 = jnp.bfloat16
LANES = 128


def round_edge(total):
    edge = 1
    while (edge + 1) ** 3 <= total:
        edge = edge + 1
    return edge


def round_up(value, unit):
    return -(-value // unit) * unit


def three(table, axis):
    high = table.astype(jnp.bfloat16)
    low = (table - high.astype(np.float64)).astype(jnp.bfloat16)
    return np.concatenate([high, high, low], axis=axis)


def angle(outer, inner, modulus):
    return 2.0 * math.pi / modulus * (np.outer(outer, inner) % modulus)


def plane_table(outputs, inputs, modulus, factor, width):
    theta = angle(outputs, inputs, modulus)
    table = np.zeros((2 * len(outputs), width))
    table[: len(outputs), : len(inputs)] = factor * np.cos(theta)
    table[len(outputs) :, : len(inputs)] = factor * np.sin(theta)
    return three(table, 1)


def depth_table(positions, count, modulus, rows, half):
    theta = angle(positions, np.arange(count), modulus)
    table = np.zeros((rows, 2 * half))
    table[: len(positions), :count] = np.cos(theta)
    table[: len(positions), half : half + count] = -np.sin(theta)
    return three(table, 0)


def depth_inverse(count, length, modulus, half):
    freqs = np.arange(count)
    theta = angle(freqs, np.arange(length), modulus)
    weight = np.where((freqs == 0) | (2 * freqs == modulus), 1.0, 2.0) / modulus
    table = np.zeros((2 * half, length))
    table[:count] = weight[:, None] * np.cos(theta)
    table[half : half + count] = -weight[:, None] * np.sin(theta)
    return three(table, 0)


def axis_tables(cells, reach, size):
    width = cells + 2 * reach
    whole = np.arange(width)
    own = reach + np.arange(cells)
    return [
        plane_table(whole, whole, width, 1.0, width),
        plane_table(whole, np.arange(size) - reach, width, 1.0, width),
        plane_table(whole, own, width, 1.0, cells),
        plane_table(own, whole, width, 1.0 / width, width),
        plane_table(whole, whole, width, 1.0 / width, width),
    ]


def split3(x, axis):
    high = x.astype(BF16)
    low = (x - high.astype(F32)).astype(BF16)
    return jnp.concatenate([high, low, high], axis=axis)


def along_depth(x, table):
    return jnp.dot(split3(x, 1), table, preferred_element_type=F32)


def along_plane(x, table, inverse):
    both = jnp.dot(table, split3(x, 0), preferred_element_type=F32)
    count, half = both.shape[0] // 2, both.shape[1] // 2
    direct, crossed = both[:count], both[count:]
    real, imag = crossed[:, :half], crossed[:, half:]
    if inverse:
        return direct[:, :half] - imag, direct[:, half:] + real
    return direct[:, :half] + imag, direct[:, half:] - real


def body(
    nx, ny, reach, size,
    est, rec, cube, back, tz, tzk, tzi,
    xf, xk, xo, xc, xw, yf, yk, yo, yc, yw,
    out,
    win, spec, work, s3, quot, s2b, ow, rx, ry, pkx, pky,
    send, recv, sendx, recvx, sendy, recvy,
):
    views = rec.shape[0]
    cx, cy, depth = est.shape
    wx, wy = cx + 2 * reach, cy + 2 * reach
    half = tz.shape[1] // 2
    gx, gy = lax.axis_index("gx"), lax.axis_index("gy")
    right, left = {"gx": lax.rem(gx + 1, nx)}, {"gx": lax.rem(gx + nx - 1, nx)}
    above, below = {"gy": lax.rem(gy + 1, ny)}, {"gy": lax.rem(gy + ny - 1, ny)}
    has = {"right": gx < nx - 1, "left": gx > 0, "above": gy < ny - 1, "below": gy > 0}

    barrier = pltpu.get_barrier_semaphore()
    for d in range(1, nx):
        pl.semaphore_signal(
            barrier, inc=1, device_id={"gx": lax.rem(gx + d, nx)}, device_id_type=pl.DeviceIdType.MESH
        )
    for d in range(1, ny):
        pl.semaphore_signal(
            barrier, inc=1, device_id={"gy": lax.rem(gy + d, ny)}, device_id_type=pl.DeviceIdType.MESH
        )
    pl.semaphore_wait(barrier, nx + ny - 2)

    def copy(src, dst, k, target):
        return pltpu.make_async_remote_copy(
            src_ref=src, dst_ref=dst, send_sem=send.at[k], recv_sem=recv.at[k],
            device_id=target, device_id_type=pl.DeviceIdType.MESH,
        )

    def start(c, to):
        @pl.when(has[to])
        def _():
            c.start()

    def wait_send(c, to):
        @pl.when(has[to])
        def _():
            c.wait_send()

    def wait_recv(c, source):
        @pl.when(has[source])
        def _():
            c.wait_recv()

    hx, hy = pl.ds(reach, cx), pl.ds(reach, cy)
    low, high_x, high_y = pl.ds(0, reach), pl.ds(reach + cx, reach), pl.ds(reach + cy, reach)
    last_x, first = pl.ds(cx, reach), pl.ds(reach, reach)
    y_up = copy(est.at[:, pl.ds(cy - reach, reach)], win.at[hx, low], 0, above)
    y_down = copy(est.at[:, low], win.at[hx, high_y], 1, below)
    x_up = [copy(est.at[pl.ds(cx - reach, reach)], win.at[low, hy], 2, right)]
    x_down = [copy(est.at[low], win.at[high_x, hy], 3, left)]
    for n, strip in enumerate((low, high_y)):
        x_up.append(copy(win.at[last_x, strip], win.at[low, strip], 4 + 2 * n, right))
        x_down.append(copy(win.at[first, strip], win.at[high_x, strip], 5 + 2 * n, left))
    start(y_up, "above")
    start(y_down, "below")
    start(x_up[0], "right")
    start(x_down[0], "left")

    win[hx, hy] = est[...]

    @pl.when(gy == 0)
    def _():
        win[hx, low] = jnp.zeros((cx, reach, depth), F32)

    @pl.when(gy == ny - 1)
    def _():
        win[hx, high_y] = jnp.zeros((cx, reach, depth), F32)

    @pl.when(gx == 0)
    def _():
        win[low] = jnp.zeros((reach, wy, depth), F32)

    @pl.when(gx == nx - 1)
    def _():
        win[high_x] = jnp.zeros((reach, wy, depth), F32)

    def put(ref, index, rows, pair):
        ref[index + (0, rows)] = pair[0]
        ref[index + (1, rows)] = pair[1]

    def get(ref, index, rows):
        return jnp.concatenate([ref[index + (0, rows)], ref[index + (1, rows)]], axis=1)

    step = math.gcd(wx, 8)

    def depth_then_y(load, count, table, plane):
        def go(c, carry):
            spectrum = along_depth(load(c), table)
            for n in range(step):
                pair = along_plane(spectrum[n * wy : (n + 1) * wy], plane, False)
                put(work, (), pl.ds(pl.multiple_of((c * step + n) * wy, 8), wy), pair)
            return carry

        lax.fori_loop(0, count, go, 0)

    def kernel_spectrum(v):
        blocks = -(-size // step)
        scale = 1.0 / jnp.sum(cube[v])
        depth_then_y(
            lambda c: cube[v, pl.ds(pl.multiple_of(c * step * wy, 8), step * wy)], blocks, tzk[...], yk[...]
        )
        rest = wx * wy - blocks * step * wy
        if rest:
            for h in range(2):
                work[h, pl.ds(blocks * step * wy, rest)] = jnp.zeros((rest, half), F32)

        def go(q, carry):
            pair = along_plane(get(work, (), pl.ds(q, wx, stride=wy)), xk[...], False)
            pair = (pair[0] * scale, pair[1] * scale)
            put(spec, (v,), pl.ds(pl.multiple_of(q * wx, 8), wx), pair)
            return carry

        lax.fori_loop(0, wy, go, 0, unroll=4)

    kernel_spectrum(0)

    wait_recv(y_up, "below")
    wait_recv(y_down, "above")
    for c in x_up[1:]:
        start(c, "right")
    for c in x_down[1:]:
        start(c, "left")

    for v in range(1, views):
        kernel_spectrum(v)

    for c in x_up:
        wait_recv(c, "left")
    for c in x_down:
        wait_recv(c, "right")

    depth_then_y(
        lambda c: win[pl.ds(c * step, step)].reshape(step * wy, depth), wx // step, tz[...], yf[...]
    )

    def filter_forward(q, carry):
        real, imag = along_plane(get(work, (), pl.ds(q, wx, stride=wy)), xf[...], False)
        rows = pl.ds(pl.multiple_of(q * wx, 8), wx)
        for v in range(views):
            kr, ki = spec[v, 0, rows], spec[v, 1, rows]
            product = jnp.concatenate([real * kr - imag * ki, real * ki + imag * kr], axis=1)
            put(s3, (v,), pl.ds(pl.multiple_of(q * cx, 8), cx), along_plane(product, xc[...], True))
        return carry

    lax.fori_loop(0, wy, filter_forward, 0, unroll=4)

    tops = jnp.zeros((8, depth), F32)
    for v in range(views):
        planes = []
        for x in range(cx):
            pair = along_plane(get(s3, (v,), pl.ds(x, wy, stride=cx)), yc[...], True)
            planes.append(jnp.concatenate(pair, axis=1))
        blurred = along_depth(jnp.concatenate(planes, axis=0), tzi[...]) + back[v]
        quotient = rec[v].reshape(cx * cy, depth) / blurred
        quot[v] = quotient
        top = jnp.max(quotient.reshape(cx * cy // 8, 8, depth), axis=0)
        tops = top if v == 0 else jnp.maximum(tops, top)

    def spread_peak(axis, me, count, slots, send_sems, recv_sems):
        copies = []
        for d in range(1, count):
            copies.append(
                pltpu.make_async_remote_copy(
                    src_ref=slots.at[0], dst_ref=slots.at[d], send_sem=send_sems.at[d],
                    recv_sem=recv_sems.at[d], device_id={axis: lax.rem(me + d, count)},
                    device_id_type=pl.DeviceIdType.MESH,
                )
            )
        for c in copies:
            c.start()
        for c in copies:
            c.wait()

    pkx[0] = tops
    spread_peak("gx", gx, nx, pkx, sendx, recvx)
    pky[0] = jnp.max(pkx[...], axis=0)
    spread_peak("gy", gy, ny, pky, sendy, recvy)
    limit = clip_fraction * jnp.max(jnp.max(pky[...], axis=0))

    for v in range(views):
        spectrum = along_depth(jnp.minimum(quot[v], limit), tz[...])
        for x in range(cx):
            pair = along_plane(spectrum[x * cy : (x + 1) * cy], yo[...], False)
            put(s2b, (v,), pl.ds(x * wy, wy), pair)

    def filter_back(q, carry):
        rows = pl.ds(pl.multiple_of(q * wx, 8), wx)
        real = imag = None
        for v in range(views):
            ar, ai = along_plane(get(s2b, (v,), pl.ds(q, cx, stride=wy)), xo[...], False)
            kr, ki = spec[v, 0, rows], spec[v, 1, rows]
            pr, pi = ar * kr + ai * ki, ai * kr - ar * ki
            real, imag = (pr, pi) if v == 0 else (real + pr, imag + pi)
        put(work, (), rows, along_plane(jnp.concatenate([real, imag], axis=1), xw[...], True))
        return carry

    lax.fori_loop(0, wy, filter_back, 0, unroll=4)

    few = math.gcd(math.gcd(reach, cx), 8)

    def finish_slab(begin, count):
        def go(c, carry):
            planes = []
            for n in range(few):
                pair = along_plane(get(work, (), pl.ds(begin + c * few + n, wy, stride=wx)), yw[...], True)
                planes.append(jnp.concatenate(pair, axis=1))
            volume = along_depth(jnp.concatenate(planes, axis=0), tzi[...])
            ow[pl.ds(begin + c * few, few)] = volume.reshape(few, wy, depth)
            return carry

        lax.fori_loop(0, count // few, go, 0)

    to_left = copy(ow.at[low], rx.at[0], 8, left)
    to_right = copy(ow.at[high_x], rx.at[1], 9, right)
    to_below = copy(ow.at[hx, low], ry.at[0], 10, below)
    to_above = copy(ow.at[hx, high_y], ry.at[1], 11, above)
    finish_slab(0, reach)
    start(to_left, "left")
    finish_slab(reach + cx, reach)
    start(to_right, "right")
    finish_slab(reach, cx)

    @pl.when(has["right"])
    def _():
        to_left.wait_recv()
        ow[last_x] = ow[last_x] + rx[0]

    @pl.when(has["left"])
    def _():
        to_right.wait_recv()
        ow[first] = ow[first] + rx[1]

    start(to_below, "below")
    start(to_above, "above")

    @pl.when(has["above"])
    def _():
        to_below.wait_recv()
        ow[hx, pl.ds(cy, reach)] = ow[hx, pl.ds(cy, reach)] + ry[0]

    @pl.when(has["below"])
    def _():
        to_above.wait_recv()
        ow[hx, first] = ow[hx, first] + ry[1]

    out[...] = est[...] * (ow[hx, hy] / views)

    wait_send(y_up, "above")
    wait_send(y_down, "below")
    for c in x_up + [to_right]:
        wait_send(c, "right")
    for c in x_down + [to_left]:
        wait_send(c, "left")
    wait_send(to_below, "below")
    wait_send(to_above, "above")


def on_device(nx, ny, estimate, recorded, spread, background):
    views = spread.shape[0]
    size = round_edge(spread.shape[1])
    reach = size // 2
    cx, cy, depth = estimate.shape
    wx, wy = cx + 2 * reach, cy + 2 * reach
    period = depth + reach
    freqs = period // 2 + 1
    half = round_up(freqs, LANES)
    taps = round_up(size, LANES)
    cube = jnp.pad(
        spread.reshape(views, size, size, size),
        ((0, 0), (0, wx - size), (0, wy - size), (0, taps - size)),
    ).reshape(views, wx * wy, taps)
    tables = [
        depth_table(np.arange(depth), freqs, period, depth, half),
        depth_table(np.arange(size) - reach, freqs, period, taps, half),
        depth_inverse(freqs, depth, period, half),
    ]
    tables += axis_tables(cx, reach, size) + axis_tables(cy, reach, size)
    vmem = pl.BlockSpec(memory_space=pltpu.VMEM)
    smem = pl.BlockSpec(memory_space=pltpu.SMEM)
    dma = pltpu.SemaphoreType.DMA
    return pl.pallas_call(
        functools.partial(body, nx, ny, reach, size),
        out_shape=jax.ShapeDtypeStruct(estimate.shape, estimate.dtype),
        in_specs=[vmem, vmem, vmem, smem] + [vmem] * len(tables),
        out_specs=vmem,
        scratch_shapes=[
            pltpu.VMEM((wx, wy, depth), F32),
            pltpu.VMEM((views, 2, wx * wy, half), F32),
            pltpu.VMEM((2, wx * wy, half), F32),
            pltpu.VMEM((views, 2, cx * wy, half), F32),
            pltpu.VMEM((views, cx * cy, depth), F32),
            pltpu.VMEM((views, 2, cx * wy, half), F32),
            pltpu.VMEM((wx, wy, depth), F32),
            pltpu.VMEM((2, reach, wy, depth), F32),
            pltpu.VMEM((2, cx, reach, depth), F32),
            pltpu.VMEM((nx, 8, depth), F32),
            pltpu.VMEM((ny, 8, depth), F32),
            dma((12,)), dma((12,)),
            dma((nx,)), dma((nx,)),
            dma((ny,)), dma((ny,)),
        ],
        compiler_params=pltpu.CompilerParams(
            collective_id=0, has_side_effects=True, vmem_limit_bytes=60 * 1024 * 1024
        ),
    )(estimate, recorded, cube, background, *[jnp.asarray(t) for t in tables])


def solution(mesh):
    in_specs = (P("gx", "gy", None), P(None, "gx", "gy", None), P(), P())
    return jax.shard_map(
        functools.partial(on_device, mesh.shape["gx"], mesh.shape["gy"]),
        mesh=mesh, in_specs=in_specs, out_specs=P("gx", "gy", None), check_vma=False,
    )
```

profile of v0, /device:TPU:1, one launch (start us, length us, event | category | flops | bytes accessed | tf_op | source)
XLA Modules:
  0.0 72.7 jit_solution(1269903723505848822)
XLA Ops:
  0.0 1.8 %reshape.6 = f32[2,33,33,33]{3,2,1,0:T(8,128)S(1)} reshape(f32[2,35937]{1,0:T(2,128)} %param.19) | data formatting | bytes 574992 | tf_op jit(solution)/shard_map/reshape | solution.py:372
  1.8 1.6 %pad.4 = f32[2,48,48,128]{3,2,1,0:T(8,128)} pad(f32[2,33,33,33]{3,2,1,0:T(8,128)S(1)} %reshape.6, f32[]{:T(128)} %constant.18.clone.1), padding=0_0x0_15x0_15x0_95 | pad | bytes 2646796 | tf_op jit(solution)/shard_map/jit(_pad)/pad | solution.py:371
  3.3 67.8 %shard_map.163 = f32[16,16,128]{2,1,0:T(8,128)} custom-call(f32[16,16,128]{2,1,0:T(8,128)} %est.1, f32[2,16,16,128]{3,2,1,0:T(8,128)} %rec.1, f32[2,2304,128]{2,1,0:T(8,128)} %bitcast.1, f32[2]{0:T(128)} %back.1, bf16[384,256]{1,0:T(8,128)(2,1)} %constant.19.clone.tz, bf16[384,256]{1,0:T(8,128)(2,1)} %constant.20.clone.tzk, ...), custom_call_target="tpu_custom_call" | custom-call | tf_op jit(solution)/shard_map/pallas_call | solution.py:384
  71.1 1.6 %copy.19 = f32[16,16,128]{2,1,0:T(8,128)} copy(f32[16,16,128]{2,1,0:T(8,128)} %shard_map.163) | data formatting | bytes 262144
where the time goes:
time: 72.9 us; the launch traced here: 72.7 us
  Pallas kernels  67.8 us (93%)
  local copies, waits for them, and re-layouts  4.91 us (7%)
    pallas_call x1, Pallas kernels, on_device(): pl.pallas_call(functools.partial(body, nx, ny, reach, size), out_shape=ja...  67.8 us
    reshape x1, local copies, waits for them, and re-layouts, on_device(): spread.reshape(views, size, size, size)  1.76 us
    pad x1, local copies, waits for them, and re-layouts, on_device(): jnp.pad(spread.reshape(views, size, size, size), ((0, 0), (0, wx - size),...  1.57 us
    unnamed x1, local copies, waits for them, and re-layouts  1.57 us

commit v1 on v0

--- a/solution.py
+++ b/solution.py
@@ -107,6 +107,7 @@
     cx, cy, depth = est.shape
     wx, wy = cx + 2 * reach, cy + 2 * reach
     half = tz.shape[1] // 2
+    px, py, pc = wx + 1, wy + 1, cx + 1
     gx, gy = lax.axis_index("gx"), lax.axis_index("gy")
     right, left = {"gx": lax.rem(gx + 1, nx)}, {"gx": lax.rem(gx + nx - 1, nx)}
     above, below = {"gy": lax.rem(gy + 1, ny)}, {"gy": lax.rem(gy + ny - 1, ny)}
@@ -191,7 +192,7 @@
             spectrum = along_depth(load(c), table)
             for n in range(step):
                 pair = along_plane(spectrum[n * wy : (n + 1) * wy], plane, False)
-                put(work, (), pl.ds(pl.multiple_of((c * step + n) * wy, 8), wy), pair)
+                put(work, (), pl.ds((c * step + n) * py, wy), pair)
             return carry
 
         lax.fori_loop(0, count, go, 0)
@@ -202,13 +203,13 @@
         depth_then_y(
             lambda c: cube[v, pl.ds(pl.multiple_of(c * step * wy, 8), step * wy)], blocks, tzk[...], yk[...]
         )
-        rest = wx * wy - blocks * step * wy
+        rest = (wx - blocks * step) * py
         if rest:
             for h in range(2):
-                work[h, pl.ds(blocks * step * wy, rest)] = jnp.zeros((rest, half), F32)
+                work[h, pl.ds(blocks * step * py, rest)] = jnp.zeros((rest, half), F32)
 
         def go(q, carry):
-            pair = along_plane(get(work, (), pl.ds(q, wx, stride=wy)), xk[...], False)
+            pair = along_plane(get(work, (), pl.ds(q, wx, stride=py)), xk[...], False)
             pair = (pair[0] * scale, pair[1] * scale)
             put(spec, (v,), pl.ds(pl.multiple_of(q * wx, 8), wx), pair)
             return carry
@@ -237,12 +238,12 @@
     )
 
     def filter_forward(q, carry):
-        real, imag = along_plane(get(work, (), pl.ds(q, wx, stride=wy)), xf[...], False)
+        real, imag = along_plane(get(work, (), pl.ds(q, wx, stride=py)), xf[...], False)
         rows = pl.ds(pl.multiple_of(q * wx, 8), wx)
         for v in range(views):
             kr, ki = spec[v, 0, rows], spec[v, 1, rows]
             product = jnp.concatenate([real * kr - imag * ki, real * ki + imag * kr], axis=1)
-            put(s3, (v,), pl.ds(pl.multiple_of(q * cx, 8), cx), along_plane(product, xc[...], True))
+            put(s3, (v,), pl.ds(q * pc, cx), along_plane(product, xc[...], True))
         return carry
 
     lax.fori_loop(0, wy, filter_forward, 0, unroll=4)
@@ -251,7 +252,7 @@
     for v in range(views):
         planes = []
         for x in range(cx):
-            pair = along_plane(get(s3, (v,), pl.ds(x, wy, stride=cx)), yc[...], True)
+            pair = along_plane(get(s3, (v,), pl.ds(x, wy, stride=pc)), yc[...], True)
             planes.append(jnp.concatenate(pair, axis=1))
         blurred = along_depth(jnp.concatenate(planes, axis=0), tzi[...]) + back[v]
         quotient = rec[v].reshape(cx * cy, depth) / blurred
@@ -284,17 +285,17 @@
         spectrum = along_depth(jnp.minimum(quot[v], limit), tz[...])
         for x in range(cx):
             pair = along_plane(spectrum[x * cy : (x + 1) * cy], yo[...], False)
-            put(s2b, (v,), pl.ds(x * wy, wy), pair)
+            put(s2b, (v,), pl.ds(x * py, wy), pair)
 
     def filter_back(q, carry):
         rows = pl.ds(pl.multiple_of(q * wx, 8), wx)
         real = imag = None
         for v in range(views):
-            ar, ai = along_plane(get(s2b, (v,), pl.ds(q, cx, stride=wy)), xo[...], False)
+            ar, ai = along_plane(get(s2b, (v,), pl.ds(q, cx, stride=py)), xo[...], False)
             kr, ki = spec[v, 0, rows], spec[v, 1, rows]
             pr, pi = ar * kr + ai * ki, ai * kr - ar * ki
             real, imag = (pr, pi) if v == 0 else (real + pr, imag + pi)
-        put(work, (), rows, along_plane(jnp.concatenate([real, imag], axis=1), xw[...], True))
+        put(work, (), pl.ds(q * px, wx), along_plane(jnp.concatenate([real, imag], axis=1), xw[...], True))
         return carry
 
     lax.fori_loop(0, wy, filter_back, 0, unroll=4)
@@ -305,7 +306,7 @@
         def go(c, carry):
             planes = []
             for n in range(few):
-                pair = along_plane(get(work, (), pl.ds(begin + c * few + n, wy, stride=wx)), yw[...], True)
+                pair = along_plane(get(work, (), pl.ds(begin + c * few + n, wy, stride=px)), yw[...], True)
                 planes.append(jnp.concatenate(pair, axis=1))
             volume = along_depth(jnp.concatenate(planes, axis=0), tzi[...])
             ow[pl.ds(begin + c * few, few)] = volume.reshape(few, wy, depth)
@@ -313,28 +314,35 @@
 
         lax.fori_loop(0, count // few, go, 0)
 
-    to_left = copy(ow.at[low], rx.at[0], 8, left)
-    to_right = copy(ow.at[high_x], rx.at[1], 9, right)
-    to_below = copy(ow.at[hx, low], ry.at[0], 10, below)
-    to_above = copy(ow.at[hx, high_y], ry.at[1], 11, above)
+    strips = (low, high_y, hy)
+    to_left = [copy(ow.at[low, t], rx.at[0, :, t], 8 + n, left) for n, t in enumerate(strips)]
+    to_right = [copy(ow.at[high_x, t], rx.at[1, :, t], 13 + n, right) for n, t in enumerate(strips)]
+    to_below = copy(ow.at[hx, low], ry.at[0], 11, below)
+    to_above = copy(ow.at[hx, high_y], ry.at[1], 12, above)
     finish_slab(0, reach)
-    start(to_left, "left")
+    for c in to_left:
+        start(c, "left")
     finish_slab(reach + cx, reach)
-    start(to_right, "right")
+    for c in to_right:
+        start(c, "right")
     finish_slab(reach, cx)
 
-    @pl.when(has["right"])
-    def _():
-        to_left.wait_recv()
-        ow[last_x] = ow[last_x] + rx[0]
-
-    @pl.when(has["left"])
-    def _():
-        to_right.wait_recv()
-        ow[first] = ow[first] + rx[1]
-
+    def add_slabs(n):
+        @pl.when(has["right"])
+        def _():
+            to_left[n].wait_recv()
+            ow[last_x, strips[n]] = ow[last_x, strips[n]] + rx[0, :, strips[n]]
+
+        @pl.when(has["left"])
+        def _():
+            to_right[n].wait_recv()
+            ow[first, strips[n]] = ow[first, strips[n]] + rx[1, :, strips[n]]
+
+    add_slabs(0)
     start(to_below, "below")
+    add_slabs(1)
     start(to_above, "above")
+    add_slabs(2)
 
     @pl.when(has["above"])
     def _():
@@ -350,9 +358,9 @@
 
     wait_send(y_up, "above")
     wait_send(y_down, "below")
-    for c in x_up + [to_right]:
+    for c in x_up + to_right:
         wait_send(c, "right")
-    for c in x_down + [to_left]:
+    for c in x_down + to_left:
         wait_send(c, "left")
     wait_send(to_below, "below")
     wait_send(to_above, "above")
@@ -389,16 +397,16 @@
         scratch_shapes=[
             pltpu.VMEM((wx, wy, depth), F32),
             pltpu.VMEM((views, 2, wx * wy, half), F32),
-            pltpu.VMEM((2, wx * wy, half), F32),
-            pltpu.VMEM((views, 2, cx * wy, half), F32),
+            pltpu.VMEM((2, max(wx * (wy + 1), wy * (wx + 1)), half), F32),
+            pltpu.VMEM((views, 2, (cx + 1) * wy, half), F32),
             pltpu.VMEM((views, cx * cy, depth), F32),
-            pltpu.VMEM((views, 2, cx * wy, half), F32),
+            pltpu.VMEM((views, 2, cx * (wy + 1), half), F32),
             pltpu.VMEM((wx, wy, depth), F32),
             pltpu.VMEM((2, reach, wy, depth), F32),
             pltpu.VMEM((2, cx, reach, depth), F32),
             pltpu.VMEM((nx, 8, depth), F32),
             pltpu.VMEM((ny, 8, depth), F32),
-            dma((12,)), dma((12,)),
+            dma((16,)), dma((16,)),
             dma((nx,)), dma((nx,)),
             dma((ny,)), dma((ny,)),
         ],

time: 72.9 us -> 68.9 us (0.945)
  Pallas kernels: 67.8 us -> 63.8 us
    pallas_call x1, Pallas kernels: 67.8 us -> 63.8 us  [on_device(): pl.pallas_call(functools.partial(body, nx, ny, reach, size), out_shape=ja...]
where the time goes in v1:
time: 68.9 us; the launch traced here: 68.7 us
  Pallas kernels  63.8 us (93%)
  local copies, waits for them, and re-layouts  4.91 us (7%)
    pallas_call x1, Pallas kernels, on_device(): pl.pallas_call(functools.partial(body, nx, ny, reach, size), out_shape=ja...  63.8 us
    reshape x1, local copies, waits for them, and re-layouts, on_device(): spread.reshape(views, size, size, size)  1.76 us
    pad x1, local copies, waits for them, and re-layouts, on_device(): jnp.pad(spread.reshape(views, size, size, size), ((0, 0), (0, wx - size),...  1.57 us
    unnamed x1, local copies, waits for them, and re-layouts  1.57 us

profile of v1, /device:TPU:1, one launch (start us, length us, event | category | flops | bytes accessed | tf_op | source)
XLA Modules:
  0.0 68.7 jit_solution(11516497006673194032)
XLA Ops:
  0.0 1.8 %reshape.6 = f32[2,33,33,33]{3,2,1,0:T(8,128)S(1)} reshape(f32[2,35937]{1,0:T(2,128)} %param.19) | data formatting | bytes 574992 | tf_op jit(solution)/shard_map/reshape | solution.py:380
  1.8 1.6 %pad.4 = f32[2,48,48,128]{3,2,1,0:T(8,128)} pad(f32[2,33,33,33]{3,2,1,0:T(8,128)S(1)} %reshape.6, f32[]{:T(128)} %constant.18.clone.1), padding=0_0x0_15x0_15x0_95 | pad | bytes 2646796 | tf_op jit(solution)/shard_map/jit(_pad)/pad | solution.py:379
  3.3 63.8 %shard_map.163 = f32[16,16,128]{2,1,0:T(8,128)} custom-call(f32[16,16,128]{2,1,0:T(8,128)} %est.1, f32[2,16,16,128]{3,2,1,0:T(8,128)} %rec.1, f32[2,2304,128]{2,1,0:T(8,128)} %bitcast.1, f32[2]{0:T(128)} %back.1, bf16[384,256]{1,0:T(8,128)(2,1)} %constant.19.clone.tz, bf16[384,256]{1,0:T(8,128)(2,1)} %constant.20.clone.tzk, ...), custom_call_target="tpu_custom_call" | custom-call | tf_op jit(solution)/shard_map/pallas_call | solution.py:392
  67.1 1.6 %copy.19 = f32[16,16,128]{2,1,0:T(8,128)} copy(f32[16,16,128]{2,1,0:T(8,128)} %shard_map.163) | data formatting | bytes 262144
